TPU v7x, 256 devices: a whole 4x4x8 slice. The times are simulated.
256 devices in a mesh: rep: 4 (over z_hi), exp: 64 (over z_lo, x, y, core).
Axes of the slice: x: 4, y: 4, z: 8 (z_hi: 4, z_lo: 2; z = z_hi * 2 + z_lo), core: 2. Of those that a mesh axis runs over, the one named last changes fastest.
Arguments:
- act_a: bfloat16 [32768, 3584], P(('rep', 'exp')), may hold values from -6 to 6
- grad_a: bfloat16 [32768, 2, 1024], P(('rep', 'exp')), may hold values from -0.125 to 0.125
- route_a: int32 [32768, 2], P(('rep', 'exp')), may hold values from 0 to 63, all different within a row; in each aligned block of 128 rows (0 to 127, 128 to 255, ...) at most 5 rows name the same one
- act_b: bfloat16 [32768, 3584], P(('rep', 'exp')), may hold values from -6 to 6
- grad_b: bfloat16 [32768, 2, 1024], P(('rep', 'exp')), may hold values from -0.125 to 0.125
- route_b: int32 [32768, 2], P(('rep', 'exp')), may hold values from 0 to 31, all different within a row; in each aligned block of 128 rows (0 to 127, 128 to 255, ...) at most 10 rows name the same one
Outputs:
- wgrad_a: bfloat16 [64, 3584, 1024], P('exp', 'rep')
- wgrad_b: bfloat16 [64, 1792, 1024], P('exp', 'rep')
Inputs may be any that keep to these rules, and one draw needn't show every extreme that they name: `route_a`: each token names 2 different experts of layer A; the 128 tokens of one device name any one expert at most 5 times. `route_b`: each token names 2 different experts of layer B; the 128 tokens of one device name any one expert at most 2 * 5 times.
All inputs are finite; a program needn't handle non-finite values.
Results may differ from a plain program's by a relative error of at most 0.013.
Values may be sent and summed in bfloat16 or wider, within the bound.
No kernel may reach another device: no remote copies, remote signals or barrier semaphores. Data moves between devices by JAX's collectives and lax.ppermute only.
A program may use at most 128 MiB of HBM per device.

v0:
```python
import jax
import jax.numpy as jnp
from jax import lax
from jax.sharding import PartitionSpec as P


def sent_together(arrays, axis, split_dim, concat_dim, along):
    ends, at = ([], 0)
    for a in arrays[:-1]:
        at += a.shape[along]
        ends.append(at)
    both = jnp.concatenate(arrays, axis=along)
    return tuple(
        jnp.split(
            lax.all_to_all(both, axis, split_axis=split_dim, concat_axis=concat_dim, tiled=True),
            ends,
            axis=along,
        )
    )


def sent_to_all(array, axis):
    size = lax.axis_size(axis)
    return lax.all_to_all(
        jnp.broadcast_to(array[None], (size, *array.shape)), axis, 0, 0, tiled=True
    )


def joined_along(parts, dim):
    parts = jnp.moveaxis(parts, 0, dim)
    dims = parts.shape
    return parts.reshape(*dims[:dim], dims[dim] * dims[dim + 1], *dims[dim + 2 :])


def gather_directly(array, axis, dim):
    parts = sent_to_all(array, axis)
    return joined_along(parts, dim)


def from_partner(block, axis, apart):
    count = lax.axis_size(axis)
    route = []
    for low in range(count):
        high = low | 1 << apart
        if high != low and high < count:
            route += [(low, high), (high, low)]
    return lax.ppermute(block, axis, route)


def slot_sources(route, experts, stride, slot_count):
    flat_ids = route.reshape(-1)
    onehot = (flat_ids[:, None] == jnp.arange(experts, dtype=jnp.int32)[None, :]).astype(jnp.int32)
    before = jnp.cumsum(onehot, axis=0) - onehot
    position = jnp.sum(before * onehot, axis=1)
    slot_index = flat_ids * stride + position
    pair_ids = jnp.arange(flat_ids.shape[0], dtype=jnp.int32)
    return jnp.full((slot_count,), -1, jnp.int32).at[slot_index].set(pair_ids)


def fill_rows(acts, grads, sources, top_count):
    filled = (sources >= 0)[:, None]
    clamped = jnp.maximum(sources, 0)
    rows_act = jnp.where(filled, acts[clamped // top_count], jnp.zeros((), acts.dtype))
    flat_grads = grads.reshape(-1, grads.shape[-1])
    rows_grad = jnp.where(filled, flat_grads[clamped], jnp.zeros((), grads.dtype))
    return (rows_act, rows_grad)


def contract(left, right):
    return lax.dot_general(
        left, right, (((0,), (0,)), ((), ())), preferred_element_type=jnp.float32
    )


def shards(act_a, grad_a, route_a, act_b, grad_b, route_b):
    exp_count = lax.axis_size("exp")
    token_count = act_a.shape[0]
    top_count = route_a.shape[1]
    features = act_a.shape[1]
    hidden = grad_a.shape[2]
    most_rows = token_count * top_count * 5 // (4 * exp_count)
    sources_a = slot_sources(route_a, exp_count, most_rows, exp_count * most_rows)
    send_act, send_grad = fill_rows(act_a, grad_a, sources_a, top_count)
    recv_act, recv_grad = sent_together((send_act, send_grad), "exp", 0, 0, 1)
    columns_mine = lax.all_to_all(recv_act, "rep", split_axis=1, concat_axis=0, tiled=True)
    owned_a = contract(columns_mine, gather_directly(recv_grad, "rep", 0))
    wgrad_a = owned_a.astype(jnp.bfloat16)[None]
    half_exp = exp_count // 2
    sources_b = slot_sources(route_b, half_exp, 2 * most_rows, exp_count * most_rows)
    send_act_b, send_grad_b = fill_rows(act_b, grad_b, sources_b, top_count)
    recv_act_b, recv_grad_b = sent_together((send_act_b, send_grad_b), "exp", 0, 0, 1)
    partial_value = (
        contract(recv_act_b, recv_grad_b).astype(jnp.bfloat16).reshape(2, features // 2, hidden)
    )
    parity = lax.axis_index("exp") % 2
    kept_half = lax.dynamic_index_in_dim(partial_value, parity, 0, keepdims=False)
    sent_half = lax.dynamic_index_in_dim(partial_value, 1 - parity, 0, keepdims=False)
    arrived = from_partner(sent_half, "exp", 0)
    paired = (kept_half.astype(jnp.float32) + arrived.astype(jnp.float32)).astype(jnp.bfloat16)
    owned_b = lax.psum_scatter(paired, "rep", scatter_dimension=0, tiled=True).astype(jnp.float32)
    wgrad_b = owned_b.astype(jnp.bfloat16)[None]
    return (wgrad_a, wgrad_b)


def solution(mesh):
    return jax.shard_map(
        shards,
        mesh=mesh,
        in_specs=(
            P(("rep", "exp"), None),
            P(("rep", "exp"), None, None),
            P(("rep", "exp"), None),
            P(("rep", "exp"), None),
            P(("rep", "exp"), None, None),
            P(("rep", "exp"), None),
        ),
        out_specs=(P("exp", "rep", None), P("exp", "rep", None)),
        check_vma=False,
    )
```

profile of v0, /device:TPU:34, one launch (start us, length us, event | category | flops | bytes accessed | tf_op | source)
XLA Modules:
  0.0 382.3 jit_solution(356382941867029190)
XLA Ops:
  7.2 0.0 copy-start
  7.2 0.9 copy.14
  8.0 0.1 eq.64
  8.2 0.1 eq.60
  8.3 0.7 broadcast_multiply_fusion
  9.0 0.6 reduce-window.16
  9.6 0.2 slice_reduce_fusion.1
  9.8 0.1 copy.13
  10.0 0.1 mul.44
  10.1 0.1 fusion.14
  10.2 1.4 scatter_custom_fusion.1
  11.7 0.0 copy-done
  11.7 3.1 gather_fusion.2
  14.8 2.7 gather.25
  17.5 0.1 broadcast_in_dim.79
  17.6 1.2 reshape.147
  18.9 2.1 gather_fusion.3
  21.0 0.3 gather.27
  21.3 2.4 broadcast_select_fusion
  23.7 0.2 broadcast_select_fusion.2
  23.9 3.0 pad_maximum_fusion.1
  26.9 9.4 %all-to-all-start.3 = ((bf16[64,5,4608]{2,1,0:T(8,128)(2,1)}), bf16[64,5,4608]{2,1,0:T(8,128)(2,1)}, u32[]{:S(2)}, u32[]{:S(2)}) async-start(bf16[64,5,4608]{2,1,0:T(8,128)(2,1)} %pad_maximum_fusion.1), calls=%async_computation.3 | async-start | bytes 9437184 | tf_op jit(solution)/shard_map/all_to_all | solution.py:15
  36.3 0.0 copy-done.4
  36.3 0.1 copy.9
  36.4 0.1 eq.56
  36.5 0.1 eq.52
  36.7 0.6 reduce-window.14
  37.3 0.2 slice_reduce_fusion
  37.5 0.1 copy.8
  37.6 0.1 mul.40
  37.8 0.1 fusion.10
  37.9 1.6 scatter_custom_fusion
  39.5 0.0 copy-done.2
  39.5 3.1 gather_fusion
  42.7 2.7 gather.21
  45.4 0.1 broadcast_in_dim.70
  45.5 1.2 reshape.145
  46.8 2.1 gather_fusion.1
  48.9 0.3 gather.23
  49.1 0.2 broadcast_select_fusion.3
  49.3 2.4 broadcast_select_fusion.1
  51.7 3.0 pad_maximum_fusion
  54.7 40.7 %all-to-all-done.3 = bf16[64,5,4608]{2,1,0:T(8,128)(2,1)} async-done(((bf16[64,5,4608]{2,1,0:T(8,128)(2,1)}), bf16[64,5,4608]{2,1,0:T(8,128)(2,1)}, u32[]{:S(2)}, u32[]{:S(2)}) %all-to-all-start.3) | async-done | bytes 2949152 | tf_op jit(solution)/shard_map/all_to_all | solution.py:15
  95.4 8.5 %all-to-all-start = ((bf16[64,5,4608]{2,1,0:T(8,128)(2,1)}), bf16[64,5,4608]{2,1,0:T(8,128)(2,1)}, u32[]{:S(2)}, u32[]{:S(2)}) async-start(bf16[64,5,4608]{2,1,0:T(8,128)(2,1)} %pad_maximum_fusion), calls=%async_computation | async-start | bytes 9437184 | tf_op jit(solution)/shard_map/all_to_all | solution.py:15
  103.9 5.1 %all_to_all.34 = bf16[320,4608]{1,0:T(8,128)(2,1)} reshape(bf16[64,5,4608]{2,1,0:T(8,128)(2,1)} %all-to-all-done.3) | data formatting | bytes 5898240 | tf_op jit(solution)/shard_map/all_to_all | solution.py:15
  108.9 5.8 %convolution_convert_fusion = bf16[3584,1024]{1,0:T(8,128)(2,1)S(1)} fusion(bf16[320,4608]{1,0:T(8,128)(2,1)} %all_to_all.34), kind=kOutput, calls=%fused_computation.6 | convolution fusion | flops 2352480256 | bytes 10289152 | tf_op jit(solution)/shard_map/dot_general | solution.py:70
  114.7 2.5 dynamic-slice_bitcast_fusion
  117.2 1.7 copy-done.3
  118.9 0.1 collective-permute-start
  119.0 43.9 %all-to-all-done = bf16[64,5,4608]{2,1,0:T(8,128)(2,1)} async-done(((bf16[64,5,4608]{2,1,0:T(8,128)(2,1)}), bf16[64,5,4608]{2,1,0:T(8,128)(2,1)}, u32[]{:S(2)}, u32[]{:S(2)}) %all-to-all-start) | async-done | bytes 2949152 | tf_op jit(solution)/shard_map/all_to_all | solution.py:15
  163.0 5.0 %all_to_all.28 = bf16[320,4608]{1,0:T(8,128)(2,1)} reshape(bf16[64,5,4608]{2,1,0:T(8,128)(2,1)} %all-to-all-done) | data formatting | bytes 5898240 | tf_op jit(solution)/shard_map/all_to_all | solution.py:15
  168.0 1.6 slice-done
  169.6 1.6 copy.23
  171.3 7.6 %all-to-all-start.1 = ((bf16[320,4,896]{2,0,1:T(8,128)(2,1)}), bf16[320,4,896]{2,0,1:T(8,128)(2,1)S(1)}, u32[]{:S(2)}, u32[]{:S(2)}) async-start(bf16[320,4,896]{2,0,1:T(8,128)(2,1)} %bitcast.66), calls=%async_computation.1 | async-start | bytes 4587520 | tf_op jit(solution)/shard_map/all_to_all | solution.py:85
  178.8 0.0 reduce-scatter.2.cloned.1.call-start
  178.8 0.0 collective-permute-done
  178.8 6.9 %fusion = bf16[1792,1024]{1,0:T(8,128)(2,1)} fusion(bf16[1792,1024]{1,0:T(8,128)(2,1)} %collective-permute-done, bf16[2,1792,1024]{2,1,0:T(8,128)(2,1)} %bitcast.68, s32[]{:T(128)S(6)} %select_n.79), kind=kLoop, calls=%fused_computation.8 | loop fusion | flops 7340032 | bytes 11010052 | tf_op jit(solution)/shard_map/convert_element_type | solution.py:99
  185.7 0.0 reduce-scatter.2.cloned.1.call-update
  185.8 130.6 %all-to-all-done.1 = bf16[320,4,896]{2,0,1:T(8,128)(2,1)S(1)} async-done(((bf16[320,4,896]{2,0,1:T(8,128)(2,1)}), bf16[320,4,896]{2,0,1:T(8,128)(2,1)S(1)}, u32[]{:S(2)}, u32[]{:S(2)}) %all-to-all-start.1) | async-done | bytes 2293792 | tf_op jit(solution)/shard_map/all_to_all | solution.py:85
  316.3 0.0 slice-done.1
  316.3 0.3 broadcast_in_dim.77
  316.6 55.0 %all_to_all.39 = bf16[4,320,1024]{2,1,0:T(8,128)(2,1)S(1)} all-to-all(bf16[4,320,1024]{2,1,0:T(8,128)(2,1)S(1)} %broadcast_in_dim.77), channel_id=1, replica_groups=mesh['rep'=4,'exp'=64] {'rep'}, dimensions={0} | all-to-all | bytes 5242880 | tf_op jit(solution)/shard_map/all_to_all | solution.py:24
  371.7 3.8 %fusion.4 = bf16[1,896,1024]{2,1,0:T(8,128)(2,1)} fusion(bf16[4,320,1024]{2,1,0:T(8,128)(2,1)S(1)} %all_to_all.39, bf16[320,4,896]{2,0,1:T(8,128)(2,1)S(1)} %all-to-all-done.1), kind=kOutput, calls=%fused_computation.19 | convolution fusion | flops 2349727744 | bytes 6750208 | tf_op jit(solution)/shard_map/dot_general | solution.py:70
  375.5 0.0 copy-done.1
  (24 shorter events, 0.2 us)
Async XLA Ops:
  7.2 4.5 %copy-start = (bf16[128,3584]{1,0:T(8,128)(2,1)S(1)}, bf16[128,3584]{1,0:T(8,128)(2,1)}, u32[]{:S(2)}) copy-start(bf16[128,3584]{1,0:T(8,128)(2,1)} %param.9) | copy-start | bytes 2752516
  26.9 9.4 %copy-start.4 = (s32[128,2]{0,1:T(2,128)S(1)}, s32[128,2]{0,1:T(2,128)}, u32[]{:S(2)}) copy-start(s32[128,2]{0,1:T(2,128)} %param.8) | copy-start | bytes 3076
  26.9 12.7 %copy-start.2 = (bf16[128,3584]{1,0:T(8,128)(2,1)S(1)}, bf16[128,3584]{1,0:T(8,128)(2,1)}, u32[]{:S(2)}) copy-start(bf16[128,3584]{1,0:T(8,128)(2,1)} %param.6) | copy-start | bytes 2752516
  26.9 68.5 %all-to-all-start.3 = ((bf16[64,5,4608]{2,1,0:T(8,128)(2,1)}), bf16[64,5,4608]{2,1,0:T(8,128)(2,1)}, u32[]{:S(2)}, u32[]{:S(2)}) async-start(bf16[64,5,4608]{2,1,0:T(8,128)(2,1)} %pad_maximum_fusion.1), calls=%async_computation.3 | async-start | bytes 9437184 | tf_op jit(solution)/shard_map/all_to_all | solution.py:15
  95.4 67.6 %all-to-all-start = ((bf16[64,5,4608]{2,1,0:T(8,128)(2,1)}), bf16[64,5,4608]{2,1,0:T(8,128)(2,1)}, u32[]{:S(2)}, u32[]{:S(2)}) async-start(bf16[64,5,4608]{2,1,0:T(8,128)(2,1)} %pad_maximum_fusion), calls=%async_computation | async-start | bytes 9437184 | tf_op jit(solution)/shard_map/all_to_all | solution.py:15
  114.7 4.2 %copy-start.3 = (bf16[3584,1024]{1,0:T(8,128)(2,1)}, bf16[3584,1024]{1,0:T(8,128)(2,1)S(1)}, u32[]{:S(2)}) copy-start(bf16[3584,1024]{1,0:T(8,128)(2,1)S(1)} %convolution_convert_fusion) | copy-start | bytes 22020100
  118.9 59.9 %collective-permute-start = (bf16[1792,1024]{1,0:T(8,128)(2,1)}, bf16[1792,1024]{1,0:T(8,128)(2,1)}, u32[]{:S(2)}, u32[]{:S(2)}) collective-permute-start(bf16[1792,1024]{1,0:T(8,128)(2,1)} %dynamic-slice_bitcast_fusion), channel_id=1, source_target_pairs={{0,1},{1,0},{2,3},{3,2},{4,5},{5,4},{6,7},{7,6},{8,9},{9,8},{10,11... | collective-permute-start | bytes 11010056 | tf_op jit(solution)/shard_map/ppermute | solution.py:47
  168.0 1.6 slice-start
  171.3 145.0 %all-to-all-start.1 = ((bf16[320,4,896]{2,0,1:T(8,128)(2,1)}), bf16[320,4,896]{2,0,1:T(8,128)(2,1)S(1)}, u32[]{:S(2)}, u32[]{:S(2)}) async-start(bf16[320,4,896]{2,0,1:T(8,128)(2,1)} %bitcast.66), calls=%async_computation.1 | async-start | bytes 4587520 | tf_op jit(solution)/shard_map/all_to_all | solution.py:85
  178.8 196.7 %reduce-scatter.2.cloned.1.call-start = ((), (), s32[]{:S(2)}) async-start(), calls=%async_computation.5 | async-start | bytes 4587520 | tf_op jit(solution)/shard_map/reduce_scatter | solution.py:100
  185.7 130.6 %slice-start.1 = ((bf16[320,4608]{1,0:T(8,128)(2,1)}), bf16[320,1024]{1,0:T(8,128)(2,1)S(1)}, s32[]{:S(2)}) async-start(bf16[320,4608]{1,0:T(8,128)(2,1)} %all_to_all.28), calls=%async_computation.7 | async-start | bytes 1310720 | tf_op jit(solution)/shard_map/split | solution.py:14
  371.7 3.8 %copy-start.1 = (bf16[128,3584]{1,0:T(8,128)(2,1)S(1)}, bf16[128,3584]{1,0:T(8,128)(2,1)}, u32[]{:S(2)}) copy-start(bf16[128,3584]{1,0:T(8,128)(2,1)} %param.9) | copy-start | bytes 2752516
Sparse Core Ops, SparseCore 0:
  185.9 157.8 reduce-scatter.1
where the time goes:
time: 383 us; the launch traced here: 382 us
  waiting for transfers between devices  215 us (56%)
  blocking collectives  55 us (14%)
  local copies, waits for them, and re-layouts  42.4 us (11%)
  starting transfers between devices  25.5 us (7%)
  other arithmetic  20.3 us (5%)
  between operations  14.3 us (4%)
  matrix products  9.63 us (3%)
    all_to_all x1, waiting for transfers between devices, shards(): lax.all_to_all(recv_act, 'rep', split_axis=1, concat_axis=0, tiled=True)  131 us
    all_to_all x2, waiting for transfers between devices, sent_together(): lax.all_to_all(both, axis, split_axis=split_dim, concat_axis=concat_dim,...  84.6 us
    all_to_all x1, blocking collectives, sent_to_all(): lax.all_to_all(jnp.broadcast_to(array[None], (size, *array.shape)), axis,...  55 us
    all_to_all x2, starting transfers between devices, sent_together(): lax.all_to_all(both, axis, split_axis=split_dim, concat_axis=concat_dim,...  17.8 us
    gather x4, local copies, waits for them, and re-layouts, fill_rows(): acts[clamped // top_count]  11.6 us
    all_to_all x2, local copies, waits for them, and re-layouts, sent_together(): lax.all_to_all(both, axis, split_axis=split_dim, concat_axis=concat_dim,...  10.1 us
    dot_general x2, matrix products, contract(): lax.dot_general(left, right, (((0,), (0,)), ((), ())), preferred_element_...  9.63 us
  transfers between devices with their start and end apart: 5, of which 3 were waited for; matrix products, arithmetic and copies ran while one was open for 10% of the time, Pallas kernels for 0%

commit v1 on v0

--- a/solution.py
+++ b/solution.py
@@ -82,7 +82,10 @@
     sources_a = slot_sources(route_a, exp_count, most_rows, exp_count * most_rows)
     send_act, send_grad = fill_rows(act_a, grad_a, sources_a, top_count)
     recv_act, recv_grad = sent_together((send_act, send_grad), "exp", 0, 0, 1)
-    columns_mine = lax.all_to_all(recv_act, "rep", split_axis=1, concat_axis=0, tiled=True)
+    columns_mine = jnp.concatenate(
+        lax.all_to_all(jnp.stack(jnp.split(recv_act, lax.axis_size("rep"), axis=1)), "rep", 0, 0),
+        axis=0,
+    )
     owned_a = contract(columns_mine, gather_directly(recv_grad, "rep", 0))
     wgrad_a = owned_a.astype(jnp.bfloat16)[None]
     half_exp = exp_count // 2

time: 383 us -> 383 us (level)
  transfers between devices with their start and end apart: 5 -> 5, of which waited for: 3 -> 3; matrix products, arithmetic and copies ran while one was open for 10% -> 11% of each run, Pallas kernels for 0% -> 0%
where the time goes in v1:
time: 383 us
  waiting for transfers between devices  215 us (56%)
  blocking collectives  55 us (14%)
  local copies, waits for them, and re-layouts  40.9 us (11%)
  starting transfers between devices  25.5 us (7%)
  other arithmetic  22.1 us (6%)
  between operations  14.3 us (4%)
  matrix products  9.62 us (3%)
    all_to_all x1, waiting for transfers between devices, shards(): lax.all_to_all(jnp.stack(jnp.split(recv_act, lax.axis_size('rep'), axis=1...  131 us
    all_to_all x2, waiting for transfers between devices, sent_together(): lax.all_to_all(both, axis, split_axis=split_dim, concat_axis=concat_dim,...  84.6 us
    all_to_all x1, blocking collectives, sent_to_all(): lax.all_to_all(jnp.broadcast_to(array[None], (size, *array.shape)), axis,...  55 us
    all_to_all x2, starting transfers between devices, sent_together(): lax.all_to_all(both, axis, split_axis=split_dim, concat_axis=concat_dim,...  17.8 us
    gather x4, local copies, waits for them, and re-layouts, fill_rows(): acts[clamped // top_count]  11.6 us
    all_to_all x2, local copies, waits for them, and re-layouts, sent_together(): lax.all_to_all(both, axis, split_axis=split_dim, concat_axis=concat_dim,...  10.1 us
    dot_general x2, matrix products, contract(): lax.dot_general(left, right, (((0,), (0,)), ((), ())), preferred_element_...  9.62 us
  transfers between devices with their start and end apart: 5, of which 3 were waited for; matrix products, arithmetic and copies ran while one was open for 11% of the time, Pallas kernels for 0%

profile of v1, /device:TPU:34, one launch (start us, length us, event | category | flops | bytes accessed | tf_op | source)
XLA Modules:
  0.0 382.6 jit_solution(11966342506521808380)
XLA Ops:
  7.2 0.0 copy-start
  7.2 0.9 copy.13
  8.0 0.1 eq.64
  8.2 0.1 eq.60
  8.3 0.7 broadcast_multiply_fusion
  9.0 0.6 reduce-window.16
  9.6 0.2 slice_reduce_fusion.1
  9.8 0.1 copy.12
  10.0 0.1 mul.44
  10.1 0.1 fusion.10
  10.2 1.4 scatter_custom_fusion.1
  11.7 0.0 copy-done
  11.7 3.1 gather_fusion.2
  14.8 2.7 gather.25
  17.5 0.1 broadcast_in_dim.79
  17.6 1.2 reshape.145
  18.9 2.1 gather_fusion.3
  21.0 0.3 gather.27
  21.3 2.4 broadcast_select_fusion
  23.7 0.2 broadcast_select_fusion.2
  23.9 3.0 pad_maximum_fusion.1
  26.9 9.4 %all-to-all-start.3 = ((bf16[64,5,4608]{2,1,0:T(8,128)(2,1)}), bf16[64,5,4608]{2,1,0:T(8,128)(2,1)}, u32[]{:S(2)}, u32[]{:S(2)}) async-start(bf16[64,5,4608]{2,1,0:T(8,128)(2,1)} %pad_maximum_fusion.1), calls=%async_computation.3 | async-start | bytes 9437184 | tf_op jit(solution)/shard_map/all_to_all | solution.py:15
  36.3 0.0 copy-done.4
  36.3 0.1 copy.9
  36.4 0.1 eq.56
  36.5 0.1 eq.52
  36.7 0.6 reduce-window.14
  37.3 0.2 slice_reduce_fusion
  37.5 0.1 copy.8
  37.6 0.1 mul.40
  37.8 0.1 fusion.6
  37.9 1.6 scatter_custom_fusion
  39.5 0.0 copy-done.2
  39.5 3.1 gather_fusion
  42.7 2.7 gather.21
  45.4 0.1 broadcast_in_dim.70
  45.5 1.2 reshape.143
  46.8 2.1 gather_fusion.1
  48.9 0.3 gather.23
  49.1 0.2 broadcast_select_fusion.3
  49.3 2.4 broadcast_select_fusion.1
  51.7 3.0 pad_maximum_fusion
  54.7 40.7 %all-to-all-done.3 = bf16[64,5,4608]{2,1,0:T(8,128)(2,1)} async-done(((bf16[64,5,4608]{2,1,0:T(8,128)(2,1)}), bf16[64,5,4608]{2,1,0:T(8,128)(2,1)}, u32[]{:S(2)}, u32[]{:S(2)}) %all-to-all-start.3) | async-done | bytes 2949152 | tf_op jit(solution)/shard_map/all_to_all | solution.py:15
  95.4 8.5 %all-to-all-start = ((bf16[64,5,4608]{2,1,0:T(8,128)(2,1)}), bf16[64,5,4608]{2,1,0:T(8,128)(2,1)}, u32[]{:S(2)}, u32[]{:S(2)}) async-start(bf16[64,5,4608]{2,1,0:T(8,128)(2,1)} %pad_maximum_fusion), calls=%async_computation | async-start | bytes 9437184 | tf_op jit(solution)/shard_map/all_to_all | solution.py:15
  103.9 5.1 %all_to_all.23 = bf16[320,4608]{1,0:T(8,128)(2,1)} reshape(bf16[64,5,4608]{2,1,0:T(8,128)(2,1)} %all-to-all-done.3) | data formatting | bytes 5898240 | tf_op jit(solution)/shard_map/all_to_all | solution.py:15
  108.9 5.8 %convolution_convert_fusion = bf16[3584,1024]{1,0:T(8,128)(2,1)S(1)} fusion(bf16[320,4608]{1,0:T(8,128)(2,1)} %all_to_all.23), kind=kOutput, calls=%fused_computation.6 | convolution fusion | flops 2352480256 | bytes 10289152 | tf_op jit(solution)/shard_map/dot_general | solution.py:70
  114.7 0.0 copy-start.3
  114.7 2.5 dynamic-slice_bitcast_fusion
  117.2 1.7 copy-done.3
  118.9 0.1 collective-permute-start
  119.0 43.9 %all-to-all-done = bf16[64,5,4608]{2,1,0:T(8,128)(2,1)} async-done(((bf16[64,5,4608]{2,1,0:T(8,128)(2,1)}), bf16[64,5,4608]{2,1,0:T(8,128)(2,1)}, u32[]{:S(2)}, u32[]{:S(2)}) %all-to-all-start) | async-done | bytes 2949152 | tf_op jit(solution)/shard_map/all_to_all | solution.py:15
  163.0 5.0 %all_to_all.19 = bf16[320,4608]{1,0:T(8,128)(2,1)} reshape(bf16[64,5,4608]{2,1,0:T(8,128)(2,1)} %all-to-all-done) | data formatting | bytes 5898240 | tf_op jit(solution)/shard_map/all_to_all | solution.py:15
  168.0 1.8 slice_bitcast_fusion.3
  169.7 1.8 pad_maximum_fusion.2
  171.5 7.6 %all-to-all-start.1 = ((bf16[4,320,896]{2,1,0:T(8,128)(2,1)}), bf16[4,320,896]{2,1,0:T(8,128)(2,1)S(1)}, u32[]{:S(2)}, u32[]{:S(2)}) async-start(bf16[4,320,896]{2,1,0:T(8,128)(2,1)} %pad_maximum_fusion.2), calls=%async_computation.1 | async-start | bytes 4587520 | tf_op jit(solution)/shard_map/all_to_all | solution.py:86
  179.1 0.0 reduce-scatter.2.cloned.1.call-start
  179.1 0.0 collective-permute-done
  179.1 6.9 %fusion = bf16[1792,1024]{1,0:T(8,128)(2,1)} fusion(bf16[1792,1024]{1,0:T(8,128)(2,1)} %collective-permute-done, bf16[2,1792,1024]{2,1,0:T(8,128)(2,1)} %bitcast.66, s32[]{:T(128)S(6)} %select_n.79), kind=kLoop, calls=%fused_computation.8 | loop fusion | flops 7340032 | bytes 11010052 | tf_op jit(solution)/shard_map/convert_element_type | solution.py:102
  186.0 0.0 reduce-scatter.2.cloned.1.call-update
  186.0 130.6 %all-to-all-done.1 = bf16[4,320,896]{2,1,0:T(8,128)(2,1)S(1)} async-done(((bf16[4,320,896]{2,1,0:T(8,128)(2,1)}), bf16[4,320,896]{2,1,0:T(8,128)(2,1)S(1)}, u32[]{:S(2)}, u32[]{:S(2)}) %all-to-all-start.1) | async-done | bytes 2293792 | tf_op jit(solution)/shard_map/all_to_all | solution.py:86
  316.6 0.0 slice-done
  316.6 0.3 broadcast_in_dim.77
  316.9 55.0 %all_to_all.28 = bf16[4,320,1024]{2,1,0:T(8,128)(2,1)S(1)} all-to-all(bf16[4,320,1024]{2,1,0:T(8,128)(2,1)S(1)} %broadcast_in_dim.77), channel_id=1, replica_groups=mesh['rep'=4,'exp'=64] {'rep'}, dimensions={0} | all-to-all | bytes 5242880 | tf_op jit(solution)/shard_map/all_to_all | solution.py:24
  371.9 3.8 %fusion.2 = bf16[1,896,1024]{2,1,0:T(8,128)(2,1)} fusion(bf16[4,320,896]{2,1,0:T(8,128)(2,1)S(1)} %all-to-all-done.1, bf16[4,320,1024]{2,1,0:T(8,128)(2,1)S(1)} %all_to_all.28), kind=kOutput, calls=%fused_computation.17 | convolution fusion | flops 2349727744 | bytes 6750208 | tf_op jit(solution)/shard_map/dot_general | solution.py:70
  (23 shorter events, 0.2 us)
Async XLA Ops:
  7.2 4.5 %copy-start = (bf16[128,3584]{1,0:T(8,128)(2,1)S(1)}, bf16[128,3584]{1,0:T(8,128)(2,1)}, u32[]{:S(2)}) copy-start(bf16[128,3584]{1,0:T(8,128)(2,1)} %param.9) | copy-start | bytes 2752516
  26.9 9.4 %copy-start.4 = (s32[128,2]{0,1:T(2,128)S(1)}, s32[128,2]{0,1:T(2,128)}, u32[]{:S(2)}) copy-start(s32[128,2]{0,1:T(2,128)} %param.8) | copy-start | bytes 3076
  26.9 12.7 %copy-start.2 = (bf16[128,3584]{1,0:T(8,128)(2,1)S(1)}, bf16[128,3584]{1,0:T(8,128)(2,1)}, u32[]{:S(2)}) copy-start(bf16[128,3584]{1,0:T(8,128)(2,1)} %param.6) | copy-start | bytes 2752516
  26.9 68.5 %all-to-all-start.3 = ((bf16[64,5,4608]{2,1,0:T(8,128)(2,1)}), bf16[64,5,4608]{2,1,0:T(8,128)(2,1)}, u32[]{:S(2)}, u32[]{:S(2)}) async-start(bf16[64,5,4608]{2,1,0:T(8,128)(2,1)} %pad_maximum_fusion.1), calls=%async_computation.3 | async-start | bytes 9437184 | tf_op jit(solution)/shard_map/all_to_all | solution.py:15
  95.4 67.6 %all-to-all-start = ((bf16[64,5,4608]{2,1,0:T(8,128)(2,1)}), bf16[64,5,4608]{2,1,0:T(8,128)(2,1)}, u32[]{:S(2)}, u32[]{:S(2)}) async-start(bf16[64,5,4608]{2,1,0:T(8,128)(2,1)} %pad_maximum_fusion), calls=%async_computation | async-start | bytes 9437184 | tf_op jit(solution)/shard_map/all_to_all | solution.py:15
  114.7 4.2 %copy-start.3 = (bf16[3584,1024]{1,0:T(8,128)(2,1)}, bf16[3584,1024]{1,0:T(8,128)(2,1)S(1)}, u32[]{:S(2)}) copy-start(bf16[3584,1024]{1,0:T(8,128)(2,1)S(1)} %convolution_convert_fusion) | copy-start | bytes 22020100
  118.9 60.2 %collective-permute-start = (bf16[1792,1024]{1,0:T(8,128)(2,1)}, bf16[1792,1024]{1,0:T(8,128)(2,1)}, u32[]{:S(2)}, u32[]{:S(2)}) collective-permute-start(bf16[1792,1024]{1,0:T(8,128)(2,1)} %dynamic-slice_bitcast_fusion), channel_id=1, source_target_pairs={{0,1},{1,0},{2,3},{3,2},{4,5},{5,4},{6,7},{7,6},{8,9},{9,8},{10,11... | collective-permute-start | bytes 11010056 | tf_op jit(solution)/shard_map/ppermute | solution.py:47
  171.5 145.0 %all-to-all-start.1 = ((bf16[4,320,896]{2,1,0:T(8,128)(2,1)}), bf16[4,320,896]{2,1,0:T(8,128)(2,1)S(1)}, u32[]{:S(2)}, u32[]{:S(2)}) async-start(bf16[4,320,896]{2,1,0:T(8,128)(2,1)} %pad_maximum_fusion.2), calls=%async_computation.1 | async-start | bytes 4587520 | tf_op jit(solution)/shard_map/all_to_all | solution.py:86
  179.1 196.7 %reduce-scatter.2.cloned.1.call-start = ((), (), s32[]{:S(2)}) async-start(), calls=%async_computation.5 | async-start | bytes 4587520 | tf_op jit(solution)/shard_map/reduce_scatter | solution.py:103
  186.0 130.6 %slice-start = ((bf16[320,4608]{1,0:T(8,128)(2,1)}), bf16[320,1024]{1,0:T(8,128)(2,1)S(1)}, s32[]{:S(2)}) async-start(bf16[320,4608]{1,0:T(8,128)(2,1)} %all_to_all.19), calls=%async_computation.6 | async-start | bytes 1310720 | tf_op jit(solution)/shard_map/split | solution.py:14
  371.9 3.8 %copy-start.1 = (bf16[128,3584]{1,0:T(8,128)(2,1)S(1)}, bf16[128,3584]{1,0:T(8,128)(2,1)}, u32[]{:S(2)}) copy-start(bf16[128,3584]{1,0:T(8,128)(2,1)} %param.9) | copy-start | bytes 2752516
Sparse Core Ops, SparseCore 0:
  186.2 157.8 reduce-scatter.1
